TPU v7x, 32 devices: a whole 2x2x4 slice. The times are simulated.
32 devices in a mesh: groups: 2 (over y), tm: 4 (over z), chan: 4 (over x, core).
Axes of the slice: x: 2, y: 2, z: 4, core: 2. Of those that a mesh axis runs over, the one named last changes fastest.
Arguments:
- vis: bfloat16 [8, 128, 2, 128], P(('groups', 'chan'), 'tm'), parts along dimension 0, may hold values from -6 to 6
- row_weight: bfloat16 [8, 128, 128, 128], P(('groups', 'chan'), 'tm'), parts along dimension 0, may hold values from -4 to 4
- col_weight: bfloat16 [8, 128, 128, 256], P(('groups', 'chan'), 'tm'), parts along dimension 0, may hold values from -0.5 to 0.5
- w_bin: int32 [8, 128, 1], P(('groups', 'chan'), 'tm'), parts along dimension 0, may hold values from 0 to 3; in each aligned block of 32 rows (0 to 31, 32 to 63, ..., all dimensions but the last counted through in order) at most 16 rows name the same one
- tile_col: int32 [8, 128], P(('groups', 'chan'), 'tm'), parts along dimension 0, may hold values from 0 to 15
- w_kernel: bfloat16 [8, 512, 512], P(('groups', 'tm')), parts along dimension 0, may hold values from -0.25 to 0.25
Outputs:
- grid: float32 [8, 128, 16, 512], P(('groups', 'tm'), 'chan'), parts along dimension 0
There are 2 independent parts, one for each index of `groups`. A program takes and returns all parts, laid end to end along the dimension named above; each array names one. Nothing has to cross between parts.
Inputs may be any that keep to these rules, and one draw needn't show every extreme that they name: `w_bin`: within the blocks of one device (aligned blocks of 32 along the channel-group and block dimensions taken together), no w-plane is named more than 16 times, a bound that some block reaches.
All inputs are finite; a program needn't handle non-finite values.
Results may differ from a plain program's by a relative error of at most 0.0041.
Values may be sent and summed in bfloat16 or wider, within the bound.
A program may use at most 128 MiB of HBM per device.

v0:
```python
import jax
import jax.numpy as jnp
from jax import lax
from jax.sharding import PartitionSpec as P

QW = 256
GC = 4096


def grid_group(total, weighted, columns, targets):
    patch = jnp.einsum("ghkv,gvq->gkhq", weighted, columns, preferred_element_type=jnp.float32)
    flat = patch.reshape(patch.shape[0], -1)
    return total.at[targets].add(flat, mode="drop")


def weigh_rows(rows, visibility):
    return (
        rows.astype(jnp.float32)[:, None, :, :] * visibility.astype(jnp.float32)[:, :, None, :]
    ).astype(jnp.bfloat16)


def body(vis, row_weight, col_weight, w_bin, tile_col, w_kernel):
    planes = lax.axis_size("tm")
    count = vis.shape[1]
    rows_k = row_weight.shape[2]
    width_v = vis.shape[3]
    width_q = col_weight.shape[3]
    tile_count = GC // QW
    per_plane = 2 * count // planes
    slot_total = planes * per_plane
    turns = 4
    group_len = slot_total // turns
    bins = w_bin[0, :, 0]
    tiles = tile_col[0]
    member = (bins[:, None] == jnp.arange(planes, dtype=jnp.int32)[None, :]).astype(jnp.int32)
    before = jnp.cumsum(member, axis=0) - member
    within = jnp.sum(before * member, axis=1)
    target = bins * per_plane + within
    source = (
        jnp.full((slot_total,), count, jnp.int32).at[target].set(jnp.arange(count, dtype=jnp.int32))
    )
    filled = source < count
    picked = jnp.minimum(source, count - 1)
    slot_tile = jnp.where(filled, tiles[picked], tile_count).reshape(planes, per_plane)
    columns = jnp.take(col_weight[0], picked, axis=0).reshape(planes, per_plane, width_v, width_q)
    start = jnp.zeros((tile_count, rows_k * 2 * width_q), jnp.float32)
    rows_sent = jnp.take(row_weight[0], picked, axis=0).reshape(planes, per_plane, rows_k, width_v)
    vis_sent = jnp.take(vis[0], picked, axis=0).reshape(planes, per_plane, 2, width_v)
    got_rows, got_vis, got_columns, got_tiles = (
        lax.all_to_all(rows_sent, "tm", split_axis=0, concat_axis=0, tiled=True),
        lax.all_to_all(vis_sent, "tm", split_axis=0, concat_axis=0, tiled=True),
        lax.all_to_all(columns, "tm", split_axis=0, concat_axis=0, tiled=True),
        lax.all_to_all(slot_tile, "tm", split_axis=0, concat_axis=0, tiled=True),
    )

    def step_raw(total, group):
        rows, visibility, cols, targets = group
        return (grid_group(total, weigh_rows(rows, visibility), cols, targets), None)

    groups = (
        got_rows.reshape(turns, group_len, rows_k, width_v),
        got_vis.reshape(turns, group_len, 2, width_v),
        got_columns.reshape(turns, group_len, width_v, width_q),
        got_tiles.reshape(turns, group_len),
    )
    total, _ = lax.scan(step_raw, start, groups)
    partial_value = total.reshape(tile_count, rows_k, 2 * width_q)
    share = rows_k // lax.axis_size("chan")
    summed = lax.psum(partial_value, "chan")
    mine = lax.dynamic_slice_in_dim(summed, lax.axis_index("chan") * share, share, 1)
    rounded = mine.astype(jnp.bfloat16)
    result = jnp.einsum("tkq,qr->ktr", rounded, w_kernel[0], preferred_element_type=jnp.float32)
    return result[None]


def solution(mesh):
    in_specs = (
        P(("groups", "chan"), "tm", None, None),
        P(("groups", "chan"), "tm", None, None),
        P(("groups", "chan"), "tm", None, None),
        P(("groups", "chan"), "tm", None),
        P(("groups", "chan"), "tm"),
        P(("groups", "tm"), None, None),
    )
    out_specs = P(("groups", "tm"), "chan", None, None)
    return jax.shard_map(body, mesh=mesh, in_specs=in_specs, out_specs=out_specs, check_vma=False)
```

profile of v0, /device:TPU:1, one launch (start us, length us, event | category | flops | bytes accessed | tf_op | source)
XLA Modules:
  0.0 493.3 jit_solution(4983551968529737838)
XLA Ops:
  0.0 0.0 copy-start
  0.0 0.9 fusion.8
  0.9 0.1 reduce_window_sum.11
  0.9 0.8 select_reduce_fusion
  1.8 0.7 fusion.9
  2.4 0.7 scatter_custom_fusion.1
  3.1 1.4 gather_fusion
  4.6 0.7 all_to_all.17
  5.3 5.4 %all-to-all-start = ((s32[4,1,16]{2,1,0:T(1,128)}), s32[4,1,16]{2,1,0:T(1,128)S(1)}, u32[]{:S(2)}, u32[]{:S(2)}) async-start(s32[4,1,16]{2,1,0:T(1,128)} %bitcast.13), calls=%async_computation | async-start | bytes 4096 | tf_op jit(solution)/shard_map/all_to_all | solution.py:53
  10.7 0.1 broadcast_in_dim.53
  10.8 1.4 gather_fusion.3
  12.1 0.8 broadcast_select_fusion.2
  12.9 3.4 gather_fusion.2
  16.3 0.0 all-to-all-done
  16.3 4.5 all-to-all-start.3
  20.8 3.2 broadcast_select_fusion.1
  24.1 1.3 all-to-all-done.3
  25.3 4.4 all-to-all-start.2
  29.8 0.0 copy-done
  29.8 2.8 gather_fusion.1
  32.6 6.4 %copy.14 = bf16[64,128,256]{1,2,0:T(8,128)(2,1)} copy(bf16[64,128,256]{2,1,0:T(8,128)(2,1)} %gather_fusion.1) | data formatting | bytes 8388608 | tf_op jit(solution)/shard_map/jit(_take)/gather | solution.py:45
  39.0 4.6 broadcast_select_fusion
  43.6 34.0 %all-to-all-done.2 = bf16[4,16,128,128]{3,2,1,0:T(8,128)(2,1)} async-done(((bf16[4,16,128,128]{3,2,1,0:T(8,128)(2,1)}), bf16[4,16,128,128]{3,2,1,0:T(8,128)(2,1)}, u32[]{:S(2)}, u32[]{:S(2)}) %all-to-all-start.2) | async-done | bytes 2097184 | tf_op jit(solution)/shard_map/all_to_all | solution.py:50
  77.6 5.0 %all-to-all-start.1 = ((bf16[4,16,128,256]{2,3,1,0:T(8,128)(2,1)}), bf16[4,16,128,256]{2,3,1,0:T(8,128)(2,1)}, u32[]{:S(2)}, u32[]{:S(2)}) async-start(bf16[4,16,128,256]{2,3,1,0:T(8,128)(2,1)} %broadcast_select_fusion), calls=%async_computation.1 | async-start | bytes 8388608 | tf_op jit(solution)/shard_map/all_to_all | solution.py:52
  82.6 92.6 %all-to-all-done.1 = bf16[4,16,128,256]{2,3,1,0:T(8,128)(2,1)} async-done(((bf16[4,16,128,256]{2,3,1,0:T(8,128)(2,1)}), bf16[4,16,128,256]{2,3,1,0:T(8,128)(2,1)}, u32[]{:S(2)}, u32[]{:S(2)}) %all-to-all-start.1) | async-done | bytes 4194336 | tf_op jit(solution)/shard_map/all_to_all | solution.py:52
  175.2 2.2 broadcast_in_dim.50
  177.5 227.6 %while.10 = (s32[]{:T(128)}, f32[16,65536]{1,0:T(8,128)}, s32[4,16]{1,0:T(4,128)S(1)}, bf16[4,16,128,256]{2,3,1,0:T(8,128)(2,1)}, bf16[4,16,128,128]{3,2,1,0:T(8...) while((s32[]{:T(128)}, f32[16,65536]{1,0:T(8,128)}, s32[4,16]{1,0:T(4,128)S(1)}, ...), condition=%wide.region_5.6_spmd, body=%wide.region_3.5_spmd.sunk | while | flops 270798912 | bytes 37266200 | solution.py:66
  177.5 1.1 bitcast_convert_fusion.5
  178.6 3.9 convolution_bitcast_fusion.3
  182.5 7.2 %copy.19 = f32[16,128,2,256]{3,2,1,0:T(2,128)} copy(f32[16,128,2,256]{1,3,2,0:T(8,128)} %convolution_bitcast_fusion.3) | data formatting | bytes 8388608 | tf_op jit(solution)/shard_map/while/body/eval_jaxpr/ghkv,gvq->gkhq/transpose | solution.py:11
  189.7 6.3 %reshape.160 = f32[16,65536]{1,0:T(8,128)} reshape(f32[16,128,2,256]{3,2,1,0:T(2,128)} %copy.19) | data formatting | bytes 8388608 | tf_op jit(solution)/shard_map/while/body/eval_jaxpr/reshape | solution.py:12
  196.1 38.3 %scatter_fusion = f32[16,65536]{1,0:T(8,128)} fusion(f32[16,65536]{1,0:T(8,128)} %get-tuple-element.97, s32[16]{0:T(128)S(1)} %fusion.16, f32[16,65536]{1,0:T(8,128)} %reshape.160), kind=kCustom, calls=%fused_computation.4.clone.1 | custom fusion | flops 1048576 | bytes 12582976 | tf_op jit(solution)/shard_map/while/body/eval_jaxpr/scatter-add | solution.py:13
  234.4 1.1 bitcast_convert_fusion.5
  235.6 3.9 convolution_bitcast_fusion.3
  239.5 7.2 %copy.19 = f32[16,128,2,256]{3,2,1,0:T(2,128)} copy(f32[16,128,2,256]{1,3,2,0:T(8,128)} %convolution_bitcast_fusion.3) | data formatting | bytes 8388608 | tf_op jit(solution)/shard_map/while/body/eval_jaxpr/ghkv,gvq->gkhq/transpose | solution.py:11
  246.7 6.3 %reshape.160 = f32[16,65536]{1,0:T(8,128)} reshape(f32[16,128,2,256]{3,2,1,0:T(2,128)} %copy.19) | data formatting | bytes 8388608 | tf_op jit(solution)/shard_map/while/body/eval_jaxpr/reshape | solution.py:12
  253.0 38.0 %scatter_fusion = f32[16,65536]{1,0:T(8,128)} fusion(f32[16,65536]{1,0:T(8,128)} %get-tuple-element.97, s32[16]{0:T(128)S(1)} %fusion.16, f32[16,65536]{1,0:T(8,128)} %reshape.160), kind=kCustom, calls=%fused_computation.4.clone.1 | custom fusion | flops 1048576 | bytes 12582976 | tf_op jit(solution)/shard_map/while/body/eval_jaxpr/scatter-add | solution.py:13
  291.0 1.1 bitcast_convert_fusion.5
  292.1 3.9 convolution_bitcast_fusion.3
  296.0 7.2 %copy.19 = f32[16,128,2,256]{3,2,1,0:T(2,128)} copy(f32[16,128,2,256]{1,3,2,0:T(8,128)} %convolution_bitcast_fusion.3) | data formatting | bytes 8388608 | tf_op jit(solution)/shard_map/while/body/eval_jaxpr/ghkv,gvq->gkhq/transpose | solution.py:11
  303.2 6.3 %reshape.160 = f32[16,65536]{1,0:T(8,128)} reshape(f32[16,128,2,256]{3,2,1,0:T(2,128)} %copy.19) | data formatting | bytes 8388608 | tf_op jit(solution)/shard_map/while/body/eval_jaxpr/reshape | solution.py:12
  309.6 38.6 %scatter_fusion = f32[16,65536]{1,0:T(8,128)} fusion(f32[16,65536]{1,0:T(8,128)} %get-tuple-element.97, s32[16]{0:T(128)S(1)} %fusion.16, f32[16,65536]{1,0:T(8,128)} %reshape.160), kind=kCustom, calls=%fused_computation.4.clone.1 | custom fusion | flops 1048576 | bytes 12582976 | tf_op jit(solution)/shard_map/while/body/eval_jaxpr/scatter-add | solution.py:13
  348.2 1.1 bitcast_convert_fusion.5
  349.3 3.9 convolution_bitcast_fusion.3
  353.2 7.2 %copy.19 = f32[16,128,2,256]{3,2,1,0:T(2,128)} copy(f32[16,128,2,256]{1,3,2,0:T(8,128)} %convolution_bitcast_fusion.3) | data formatting | bytes 8388608 | tf_op jit(solution)/shard_map/while/body/eval_jaxpr/ghkv,gvq->gkhq/transpose | solution.py:11
  360.4 6.3 %reshape.160 = f32[16,65536]{1,0:T(8,128)} reshape(f32[16,128,2,256]{3,2,1,0:T(2,128)} %copy.19) | data formatting | bytes 8388608 | tf_op jit(solution)/shard_map/while/body/eval_jaxpr/reshape | solution.py:12
  366.8 38.3 %scatter_fusion = f32[16,65536]{1,0:T(8,128)} fusion(f32[16,65536]{1,0:T(8,128)} %get-tuple-element.97, s32[16]{0:T(128)S(1)} %fusion.16, f32[16,65536]{1,0:T(8,128)} %reshape.160), kind=kCustom, calls=%fused_computation.4.clone.1 | custom fusion | flops 1048576 | bytes 12582976 | tf_op jit(solution)/shard_map/while/body/eval_jaxpr/scatter-add | solution.py:13
  405.0 6.5 %copy.17 = f32[2,8,128,512]{3,2,1,0:T(8,128)} copy(f32[2,8,128,512]{3,1,2,0:T(8,128)} %bitcast.63) | data formatting | bytes 8388608
  411.6 0.0 copy-start.1
  411.6 78.7 %all-reduce.1 = bf16[16,128,512]{2,1,0:T(8,128)(2,1)} all-reduce(f32[16,128,512]{2,1,0:T(8,128)} %bitcast.66), channel_id=1, replica_groups=mesh['groups'=2,'tm'=4,'chan'=4] {'chan'}, use_global_device_ids=true, to_apply=%region_6.7 | all-reduce | flops 1048576 | bytes 6291456 | tf_op jit(solution)/shard_map/psum | solution.py:69
  490.2 0.0 copy-done.1
  490.2 1.5 convolution_bitcast_fusion.1
  491.7 1.6 copy.15
  (12 shorter events, 0.1 us)
Async XLA Ops:
  0.0 29.8 %copy-start = (bf16[1,32,128,256]{3,2,1,0:T(8,128)(2,1)S(1)}, bf16[1,32,128,256]{3,2,1,0:T(8,128)(2,1)}, u32[]{:S(2)}) copy-start(bf16[1,32,128,256]{3,2,1,0:T(8,128)(2,1)} %param.10) | copy-start | bytes 6291460
  5.3 11.0 %all-to-all-start = ((s32[4,1,16]{2,1,0:T(1,128)}), s32[4,1,16]{2,1,0:T(1,128)S(1)}, u32[]{:S(2)}, u32[]{:S(2)}) async-start(s32[4,1,16]{2,1,0:T(1,128)} %bitcast.13), calls=%async_computation | async-start | bytes 4096 | tf_op jit(solution)/shard_map/all_to_all | solution.py:53
  16.3 9.0 %all-to-all-start.3 = ((bf16[4,16,2,128]{3,2,1,0:T(2,128)(2,1)}), bf16[4,16,2,128]{3,2,1,0:T(2,128)(2,1)S(1)}, u32[]{:S(2)}, u32[]{:S(2)}) async-start(bf16[4,16,2,128]{3,2,1,0:T(2,128)(2,1)} %broadcast_select_fusion.2), calls=%async_computation.3 | async-start | bytes 65536 | tf_op jit(solution)/shard_map/all_to_all | solution.py:51
  25.3 52.3 %all-to-all-start.2 = ((bf16[4,16,128,128]{3,2,1,0:T(8,128)(2,1)}), bf16[4,16,128,128]{3,2,1,0:T(8,128)(2,1)}, u32[]{:S(2)}, u32[]{:S(2)}) async-start(bf16[4,16,128,128]{3,2,1,0:T(8,128)(2,1)} %broadcast_select_fusion.1), calls=%async_computation.2 | async-start | bytes 4194304 | tf_op jit(solution)/shard_map/all_to_all | solution.py:50
  77.6 97.6 %all-to-all-start.1 = ((bf16[4,16,128,256]{2,3,1,0:T(8,128)(2,1)}), bf16[4,16,128,256]{2,3,1,0:T(8,128)(2,1)}, u32[]{:S(2)}, u32[]{:S(2)}) async-start(bf16[4,16,128,256]{2,3,1,0:T(8,128)(2,1)} %broadcast_select_fusion), calls=%async_computation.1 | async-start | bytes 8388608 | tf_op jit(solution)/shard_map/all_to_all | solution.py:52
  411.6 78.7 %copy-start.1 = (bf16[1,512,512]{2,1,0:T(8,128)(2,1)S(1)}, bf16[1,512,512]{2,1,0:T(8,128)(2,1)}, u32[]{:S(2)}) copy-start(bf16[1,512,512]{2,1,0:T(8,128)(2,1)} %param.13) | copy-start | bytes 1572868
where the time goes:
time: 495 us; the launch traced here: 493 us
  other arithmetic  169 us (34%)
  waiting for transfers between devices  128 us (26%)
  local copies, waits for them, and re-layouts  81.2 us (16%)
  blocking collectives  78.7 us (16%)
  starting transfers between devices  19.4 us (4%)
  matrix products  17.1 us (3%)
    scatter-add x4, other arithmetic, grid_group(): return total.at[targets].add(flat, mode='drop')  153 us
    all_to_all x1, waiting for transfers between devices, body(): lax.all_to_all(columns, 'tm', split_axis=0, concat_axis=0, tiled=True)  92.6 us
    psum x1, blocking collectives, body(): summed = lax.psum(partial_value, 'chan')  78.7 us
    all_to_all x1, waiting for transfers between devices, body(): lax.all_to_all(rows_sent, 'tm', split_axis=0, concat_axis=0, tiled=True)  34 us
    transpose x4, local copies, waits for them, and re-layouts, grid_group(): jnp.einsum('ghkv,gvq->gkhq', weighted, columns, preferred_element_type=jn...  28.8 us
    reshape x4, local copies, waits for them, and re-layouts, grid_group(): flat = patch.reshape(patch.shape[0], -1)  25.2 us
    dot_general x4, matrix products, grid_group(): jnp.einsum('ghkv,gvq->gkhq', weighted, columns, preferred_element_type=jn...  15.7 us
  transfers between devices with their start and end apart: 4, of which 3 were waited for; matrix products, arithmetic and copies ran while one was open for 5% of the time, Pallas kernels for 0%

commit v1 on v0

--- a/solution.py
+++ b/solution.py
@@ -66,7 +66,12 @@
     total, _ = lax.scan(step_raw, start, groups)
     partial_value = total.reshape(tile_count, rows_k, 2 * width_q)
     share = rows_k // lax.axis_size("chan")
-    summed = lax.psum(partial_value, "chan")
+
+    def order_grid(t0):
+        value_now = jnp.sum(lax.all_gather(t0, "chan"), 0)
+        return value_now
+
+    summed = order_grid(partial_value)
     mine = lax.dynamic_slice_in_dim(summed, lax.axis_index("chan") * share, share, 1)
     rounded = mine.astype(jnp.bfloat16)
     result = jnp.einsum("tkq,qr->ktr", rounded, w_kernel[0], preferred_element_type=jnp.float32)

time: 495 us -> 545 us (1.10)
  waiting for transfers between devices: 128 us -> 234 us
  blocking collectives: 78.7 us -> 0 us
  between operations: 0.07 us -> 13.5 us
  other arithmetic: 169 us -> 178 us
    all_gather x0 -> x1, waiting for transfers between devices: none -> 106 us  [order_grid(): value_now = jnp.sum(lax.all_gather(t0, 'chan'), 0)]
    psum x1 -> x0, blocking collectives: 78.7 us -> none  [body(): summed = lax.psum(partial_value, 'chan')]
    reduce_sum x0 -> x1, other arithmetic: none -> 10.1 us  [order_grid(): value_now = jnp.sum(lax.all_gather(t0, 'chan'), 0)]
  transfers between devices with their start and end apart: 4 -> 5, of which waited for: 3 -> 4; matrix products, arithmetic and copies ran while one was open for 5% -> 4% of each run, Pallas kernels for 0% -> 0%
where the time goes in v1:
time: 545 us; the launch traced here: 543 us
  waiting for transfers between devices  234 us (43%)
  other arithmetic  178 us (33%)
  local copies, waits for them, and re-layouts  81.2 us (15%)
  starting transfers between devices  19.4 us (4%)
  matrix products  17.2 us (3%)
  between operations  13.5 us (2%)
    scatter-add x4, other arithmetic, grid_group(): return total.at[targets].add(flat, mode='drop')  152 us
    all_gather x1, waiting for transfers between devices, order_grid(): value_now = jnp.sum(lax.all_gather(t0, 'chan'), 0)  106 us
    all_to_all x1, waiting for transfers between devices, body(): lax.all_to_all(columns, 'tm', split_axis=0, concat_axis=0, tiled=True)  92.5 us
    all_to_all x1, waiting for transfers between devices, body(): lax.all_to_all(rows_sent, 'tm', split_axis=0, concat_axis=0, tiled=True)  34 us
    transpose x4, local copies, waits for them, and re-layouts, grid_group(): jnp.einsum('ghkv,gvq->gkhq', weighted, columns, preferred_element_type=jn...  28.8 us
    reshape x4, local copies, waits for them, and re-layouts, grid_group(): flat = patch.reshape(patch.shape[0], -1)  25.2 us
    dot_general x4, matrix products, grid_group(): jnp.einsum('ghkv,gvq->gkhq', weighted, columns, preferred_element_type=jn...  15.7 us
  transfers between devices with their start and end apart: 5, of which 4 were waited for; matrix products, arithmetic and copies ran while one was open for 4% of the time, Pallas kernels for 0%

profile of v1, /device:TPU:1, one launch (start us, length us, event | category | flops | bytes accessed | tf_op | source)
XLA Modules:
  0.0 542.8 jit_solution(7895779885997238812)
XLA Ops:
  6.5 0.0 copy-start
  6.5 0.9 fusion.8
  7.4 0.1 reduce_window_sum.11
  7.5 0.8 select_reduce_fusion
  8.3 0.7 fusion.9
  9.0 0.7 scatter_custom_fusion.1
  9.7 1.4 gather_fusion
  11.1 0.7 all_to_all.17
  11.8 5.4 all-to-all-start
  17.2 0.1 broadcast_in_dim.53
  17.3 1.4 gather_fusion.3
  18.7 0.8 broadcast_select_fusion.2
  19.4 3.4 gather_fusion.2
  22.8 0.0 all-to-all-done
  22.8 4.5 all-to-all-start.3
  27.3 3.2 broadcast_select_fusion.1
  30.5 1.3 all-to-all-done.3
  31.8 4.4 all-to-all-start.2
  36.3 0.0 copy-done
  36.3 2.8 gather_fusion.1
  39.1 6.4 %copy.14 = bf16[64,128,256]{1,2,0:T(8,128)(2,1)} copy(bf16[64,128,256]{2,1,0:T(8,128)(2,1)} %gather_fusion.1) | data formatting | bytes 8388608 | tf_op jit(solution)/shard_map/jit(_take)/gather | solution.py:45
  45.5 4.6 broadcast_select_fusion
  50.1 34.0 %all-to-all-done.2 = bf16[4,16,128,128]{3,2,1,0:T(8,128)(2,1)} async-done(((bf16[4,16,128,128]{3,2,1,0:T(8,128)(2,1)}), bf16[4,16,128,128]{3,2,1,0:T(8,128)(2,1)}, u32[]{:S(2)}, u32[]{:S(2)}) %all-to-all-start.2) | async-done | bytes 2097184 | tf_op jit(solution)/shard_map/all_to_all | solution.py:50
  84.1 4.8 all-to-all-start.1
  89.0 0.2 all-gather.2.cloned.1.call-start
  89.2 92.5 %all-to-all-done.1 = bf16[4,16,128,256]{2,3,1,0:T(8,128)(2,1)} async-done(((bf16[4,16,128,256]{2,3,1,0:T(8,128)(2,1)}), bf16[4,16,128,256]{2,3,1,0:T(8,128)(2,1)}, u32[]{:S(2)}, u32[]{:S(2)}) %all-to-all-start.1) | async-done | bytes 4194336 | tf_op jit(solution)/shard_map/all_to_all | solution.py:52
  181.7 2.2 broadcast_in_dim.50
  183.9 226.5 %while.10 = (s32[]{:T(128)}, f32[16,65536]{1,0:T(8,128)}, s32[4,16]{1,0:T(4,128)S(1)}, bf16[4,16,128,256]{2,3,1,0:T(8,128)(2,1)}, bf16[4,16,128,128]{3,2,1,0:T(8...) while((s32[]{:T(128)}, f32[16,65536]{1,0:T(8,128)}, s32[4,16]{1,0:T(4,128)S(1)}, ...), condition=%wide.region_5.6_spmd, body=%wide.region_3.5_spmd.sunk | while | flops 270798912 | bytes 37266200 | solution.py:66
  183.9 1.1 bitcast_convert_fusion.5
  185.1 3.9 convolution_bitcast_fusion.3
  189.0 7.2 %copy.19 = f32[16,128,2,256]{3,2,1,0:T(2,128)} copy(f32[16,128,2,256]{1,3,2,0:T(8,128)} %convolution_bitcast_fusion.3) | data formatting | bytes 8388608 | tf_op jit(solution)/shard_map/while/body/eval_jaxpr/ghkv,gvq->gkhq/transpose | solution.py:11
  196.2 6.3 %reshape.156 = f32[16,65536]{1,0:T(8,128)} reshape(f32[16,128,2,256]{3,2,1,0:T(2,128)} %copy.19) | data formatting | bytes 8388608 | tf_op jit(solution)/shard_map/while/body/eval_jaxpr/reshape | solution.py:12
  202.5 38.0 %scatter_fusion = f32[16,65536]{1,0:T(8,128)} fusion(f32[16,65536]{1,0:T(8,128)} %get-tuple-element.97, s32[16]{0:T(128)S(1)} %fusion.16, f32[16,65536]{1,0:T(8,128)} %reshape.156), kind=kCustom, calls=%fused_computation.4.clone.1 | custom fusion | flops 1048576 | bytes 12582976 | tf_op jit(solution)/shard_map/while/body/eval_jaxpr/scatter-add | solution.py:13
  240.6 1.1 bitcast_convert_fusion.5
  241.7 3.9 convolution_bitcast_fusion.3
  245.7 7.2 %copy.19 = f32[16,128,2,256]{3,2,1,0:T(2,128)} copy(f32[16,128,2,256]{1,3,2,0:T(8,128)} %convolution_bitcast_fusion.3) | data formatting | bytes 8388608 | tf_op jit(solution)/shard_map/while/body/eval_jaxpr/ghkv,gvq->gkhq/transpose | solution.py:11
  252.9 6.3 %reshape.156 = f32[16,65536]{1,0:T(8,128)} reshape(f32[16,128,2,256]{3,2,1,0:T(2,128)} %copy.19) | data formatting | bytes 8388608 | tf_op jit(solution)/shard_map/while/body/eval_jaxpr/reshape | solution.py:12
  259.2 37.7 %scatter_fusion = f32[16,65536]{1,0:T(8,128)} fusion(f32[16,65536]{1,0:T(8,128)} %get-tuple-element.97, s32[16]{0:T(128)S(1)} %fusion.16, f32[16,65536]{1,0:T(8,128)} %reshape.156), kind=kCustom, calls=%fused_computation.4.clone.1 | custom fusion | flops 1048576 | bytes 12582976 | tf_op jit(solution)/shard_map/while/body/eval_jaxpr/scatter-add | solution.py:13
  296.9 1.1 bitcast_convert_fusion.5
  298.1 3.9 convolution_bitcast_fusion.3
  302.0 7.2 %copy.19 = f32[16,128,2,256]{3,2,1,0:T(2,128)} copy(f32[16,128,2,256]{1,3,2,0:T(8,128)} %convolution_bitcast_fusion.3) | data formatting | bytes 8388608 | tf_op jit(solution)/shard_map/while/body/eval_jaxpr/ghkv,gvq->gkhq/transpose | solution.py:11
  309.2 6.3 %reshape.156 = f32[16,65536]{1,0:T(8,128)} reshape(f32[16,128,2,256]{3,2,1,0:T(2,128)} %copy.19) | data formatting | bytes 8388608 | tf_op jit(solution)/shard_map/while/body/eval_jaxpr/reshape | solution.py:12
  315.5 38.3 %scatter_fusion = f32[16,65536]{1,0:T(8,128)} fusion(f32[16,65536]{1,0:T(8,128)} %get-tuple-element.97, s32[16]{0:T(128)S(1)} %fusion.16, f32[16,65536]{1,0:T(8,128)} %reshape.156), kind=kCustom, calls=%fused_computation.4.clone.1 | custom fusion | flops 1048576 | bytes 12582976 | tf_op jit(solution)/shard_map/while/body/eval_jaxpr/scatter-add | solution.py:13
  353.8 1.1 bitcast_convert_fusion.5
  355.0 3.9 convolution_bitcast_fusion.3
  358.9 7.2 %copy.19 = f32[16,128,2,256]{3,2,1,0:T(2,128)} copy(f32[16,128,2,256]{1,3,2,0:T(8,128)} %convolution_bitcast_fusion.3) | data formatting | bytes 8388608 | tf_op jit(solution)/shard_map/while/body/eval_jaxpr/ghkv,gvq->gkhq/transpose | solution.py:11
  366.1 6.3 %reshape.156 = f32[16,65536]{1,0:T(8,128)} reshape(f32[16,128,2,256]{3,2,1,0:T(2,128)} %copy.19) | data formatting | bytes 8388608 | tf_op jit(solution)/shard_map/while/body/eval_jaxpr/reshape | solution.py:12
  372.4 38.0 %scatter_fusion = f32[16,65536]{1,0:T(8,128)} fusion(f32[16,65536]{1,0:T(8,128)} %get-tuple-element.97, s32[16]{0:T(128)S(1)} %fusion.16, f32[16,65536]{1,0:T(8,128)} %reshape.156), kind=kCustom, calls=%fused_computation.4.clone.1 | custom fusion | flops 1048576 | bytes 12582976 | tf_op jit(solution)/shard_map/while/body/eval_jaxpr/scatter-add | solution.py:13
  410.4 6.5 %copy.17 = f32[2,8,128,512]{3,2,1,0:T(8,128)} copy(f32[2,8,128,512]{3,1,2,0:T(8,128)} %bitcast.64) | data formatting | bytes 8388608
  417.0 0.0 all-gather.2.cloned.1.call-update
  417.0 0.0 copy-start.2
  417.0 105.8 %all-gather.2.cloned.1.call-done = f32[4,16,128,512]{3,2,1,0:T(8,128)} async-done(((f32[1,16,128,512]{3,2,1,0:T(8,128)}), f32[4,16,128,512]{3,2,1,0:T(8,128)}) %all-gather.2.cloned.1.call-update) | async-done | bytes 16777232 | tf_op jit(solution)/shard_map/all_gather | solution.py:71
  522.8 0.0 copy-start.1
  522.8 10.1 %reduce_sum.22 = bf16[16,128,512]{2,1,0:T(8,128)(2,1)} reduce(f32[4,16,128,512]{3,2,1,0:T(8,128)} %all-gather.2.cloned.1.call-done, f32[]{:T(128)} %constant.44.clone.1), dimensions={0}, to_apply=%region_6.7 | reduce | flops 3145728 | bytes 18874372 | tf_op jit(solution)/shard_map/reduce_sum | solution.py:71
  532.9 0.0 copy-done.2
  532.9 1.5 convolution_bitcast_fusion.1
  534.4 1.6 copy.15
  536.0 0.0 copy-done.1
  (12 shorter events, 0.1 us)
Async XLA Ops:
  6.5 29.8 %copy-start = (bf16[1,32,128,256]{3,2,1,0:T(8,128)(2,1)S(1)}, bf16[1,32,128,256]{3,2,1,0:T(8,128)(2,1)}, u32[]{:S(2)}) copy-start(bf16[1,32,128,256]{3,2,1,0:T(8,128)(2,1)} %param.10) | copy-start | bytes 6291460
  11.8 11.0 %all-to-all-start = ((s32[4,1,16]{2,1,0:T(1,128)}), s32[4,1,16]{2,1,0:T(1,128)S(1)}, u32[]{:S(2)}, u32[]{:S(2)}) async-start(s32[4,1,16]{2,1,0:T(1,128)} %bitcast.13), calls=%async_computation | async-start | bytes 4096 | tf_op jit(solution)/shard_map/all_to_all | solution.py:53
  22.8 9.0 %all-to-all-start.3 = ((bf16[4,16,2,128]{3,2,1,0:T(2,128)(2,1)}), bf16[4,16,2,128]{3,2,1,0:T(2,128)(2,1)S(1)}, u32[]{:S(2)}, u32[]{:S(2)}) async-start(bf16[4,16,2,128]{3,2,1,0:T(2,128)(2,1)} %broadcast_select_fusion.2), calls=%async_computation.3 | async-start | bytes 65536 | tf_op jit(solution)/shard_map/all_to_all | solution.py:51
  31.8 52.3 %all-to-all-start.2 = ((bf16[4,16,128,128]{3,2,1,0:T(8,128)(2,1)}), bf16[4,16,128,128]{3,2,1,0:T(8,128)(2,1)}, u32[]{:S(2)}, u32[]{:S(2)}) async-start(bf16[4,16,128,128]{3,2,1,0:T(8,128)(2,1)} %broadcast_select_fusion.1), calls=%async_computation.2 | async-start | bytes 4194304 | tf_op jit(solution)/shard_map/all_to_all | solution.py:50
  84.1 97.6 %all-to-all-start.1 = ((bf16[4,16,128,256]{2,3,1,0:T(8,128)(2,1)}), bf16[4,16,128,256]{2,3,1,0:T(8,128)(2,1)}, u32[]{:S(2)}, u32[]{:S(2)}) async-start(bf16[4,16,128,256]{2,3,1,0:T(8,128)(2,1)} %broadcast_select_fusion), calls=%async_computation.1 | async-start | bytes 8388608 | tf_op jit(solution)/shard_map/all_to_all | solution.py:52
  89.0 433.9 %all-gather.2.cloned.1.call-start = ((), (), s32[]{:S(2)}) async-start(), calls=%async_computation.4 | async-start | bytes 20971520 | tf_op jit(solution)/shard_map/all_gather | solution.py:71
  417.0 115.9 %copy-start.2 = (bf16[1,512,512]{2,1,0:T(8,128)(2,1)S(1)}, bf16[1,512,512]{2,1,0:T(8,128)(2,1)}, u32[]{:S(2)}) copy-start(bf16[1,512,512]{2,1,0:T(8,128)(2,1)} %param.13) | copy-start | bytes 1572868
  522.8 13.1 %copy-start.1 = (bf16[1,32,128,256]{3,2,1,0:T(8,128)(2,1)S(1)}, bf16[1,32,128,256]{3,2,1,0:T(8,128)(2,1)}, u32[]{:S(2)}) copy-start(bf16[1,32,128,256]{3,2,1,0:T(8,128)(2,1)} %param.10) | copy-start | bytes 6291460
Sparse Core Ops, SparseCore 0:
  417.1 105.6 all-gather.1
